TPU v7x, 16 devices: a whole 2x2x2 slice. The times are simulated.
16 devices in a mesh: row: 2 (over z), col: 8 (over y, x, core).
Axes of the slice: x: 2, y: 2, z: 2, core: 2. Of those that a mesh axis runs over, the one named last changes fastest.
Arguments:
- w_in: float32 [2, 8, 3, 512, 1024], P('row', 'col')
- w_out: float32 [2, 8, 3, 1024, 512], P('row', 'col')
- inputs: bfloat16 [2, 8, 16, 512, 512], P('row', 'col')
- targets: bfloat16 [2, 8, 16, 512, 512], P('row', 'col')
Outputs:
- output 1: float32 [2, 8, 3, 512, 1024], P('row', 'col')
- output 2: float32 [2, 8, 3, 1024, 512], P('row', 'col')
All inputs are finite; a program needn't handle non-finite values.
Results may differ from a plain program's by a relative error of at most 0.00106204.
Values are sent between devices in bfloat16 or wider.
A program may use at most 1 GiB of HBM per device.

v0:
```python
import jax
import jax.numpy as jnp
from jax import lax
from jax.sharding import PartitionSpec as P

LR_SCALE = 0.8
EPS = 1e-6
INV_SQRT2 = 0.7071067811865476
INV_SQRT_2PI = 0.3989422804014327
CONTRACT_ROWS = (((0,), (0,)), ((), ()))
CONTRACT_LAST = (((1,), (1,)), ((), ()))


def rms_norm(rows):
    return rows * lax.rsqrt(jnp.mean(rows * rows, axis=-1, keepdims=True) + EPS)


def rms_back(rows, grad_norm):
    inv_rms = lax.rsqrt(jnp.mean(rows * rows, axis=-1, keepdims=True) + EPS)
    row_dot = jnp.mean(rows * grad_norm, axis=-1, keepdims=True)
    return inv_rms * grad_norm - rows * (inv_rms * inv_rms * inv_rms) * row_dot


def gelu_exact(pre_act):
    return 0.5 * pre_act * (1.0 + lax.erf(pre_act * INV_SQRT2))


def gelu_slope(pre_act):
    return 0.5 * (1.0 + lax.erf(pre_act * INV_SQRT2)) + pre_act * jnp.exp(-0.5 * pre_act * pre_act) * INV_SQRT_2PI


def device_grads(w_in, w_out, rows_in, rows_tgt):
    layer_count = w_in.shape[0]
    hidden = rows_in
    saved_acts = []
    for layer_idx in range(layer_count):
        w1_bf = w_in[layer_idx].astype(jnp.bfloat16)
        w2_bf = w_out[layer_idx].astype(jnp.bfloat16)
        h_f32 = hidden.astype(jnp.float32)
        normed = rms_norm(h_f32).astype(jnp.bfloat16)
        pre_act = jnp.dot(normed, w1_bf, preferred_element_type=jnp.float32)
        act_bf = gelu_exact(pre_act).astype(jnp.bfloat16)
        hidden = (h_f32 + jnp.dot(act_bf, w2_bf, preferred_element_type=jnp.float32)).astype(jnp.bfloat16)
        saved_acts.append((w1_bf, w2_bf, h_f32, normed, pre_act, act_bf))
    grad_h = (hidden.astype(jnp.float32) - rows_tgt.astype(jnp.float32)) * (2.0 / rows_tgt.size)
    grads_in = [None] * layer_count
    grads_out = [None] * layer_count
    for layer_idx in reversed(range(layer_count)):
        w1_bf, w2_bf, h_f32, normed, pre_act, act_bf = saved_acts[layer_idx]
        grad_bf = grad_h.astype(jnp.bfloat16)
        grads_out[layer_idx] = lax.dot_general(act_bf, grad_bf, CONTRACT_ROWS, preferred_element_type=jnp.float32)
        d_pre = (lax.dot_general(grad_bf, w2_bf, CONTRACT_LAST, preferred_element_type=jnp.float32) * gelu_slope(pre_act)).astype(jnp.bfloat16)
        grads_in[layer_idx] = lax.dot_general(normed, d_pre, CONTRACT_ROWS, preferred_element_type=jnp.float32)
        if layer_idx > 0:
            grad_h = grad_h + rms_back(h_f32, lax.dot_general(d_pre, w1_bf, CONTRACT_LAST, preferred_element_type=jnp.float32))
    return jnp.stack(grads_in), jnp.stack(grads_out)


def solution(mesh):
    row_size = mesh.shape["row"]
    col_size = mesh.shape["col"]
    neighbour_moves = [
        ("col", [(src_idx, (src_idx + 1) % col_size) for src_idx in range(col_size)]),
        ("col", [(src_idx, (src_idx - 1) % col_size) for src_idx in range(col_size)]),
        ("row", [(src_idx, (src_idx + 1) % row_size) for src_idx in range(row_size)]),
        ("row", [(src_idx, (src_idx - 1) % row_size) for src_idx in range(row_size)]),
    ]

    def neighbour_mix(params):
        wire_copy = params.astype(jnp.bfloat16)
        mix_sum = params
        for axis_name, pair_list in neighbour_moves:
            mix_sum = mix_sum + lax.ppermute(wire_copy, axis_name, pair_list).astype(jnp.float32)
        return mix_sum / 5.0

    def device_program(w_in, w_out, inputs, targets):
        cur_in = w_in[0, 0]
        cur_out = w_out[0, 0]
        rows_all = inputs[0, 0]
        tgt_all = targets[0, 0]
        learn_rate = LR_SCALE / cur_in.shape[0]
        for window_idx in range(rows_all.shape[0] // 2):
            step_a = 2 * window_idx
            g_a_in, g_a_out = device_grads(cur_in, cur_out, rows_all[step_a], tgt_all[step_a])
            g_b_in, g_b_out = device_grads(cur_in - learn_rate * g_a_in, cur_out - learn_rate * g_a_out,
                                           rows_all[step_a + 1], tgt_all[step_a + 1])
            mixed_in = neighbour_mix(cur_in)
            mixed_out = neighbour_mix(cur_out)
            cur_in = mixed_in - learn_rate * (g_a_in + g_b_in)
            cur_out = mixed_out - learn_rate * (g_a_out + g_b_out)
        return cur_in[None, None], cur_out[None, None]

    block_spec = P("row", "col")
    return jax.shard_map(device_program, mesh=mesh,
                         in_specs=(block_spec, block_spec, block_spec, block_spec),
                         out_specs=(block_spec, block_spec), check_vma=False)
```

profile of v0, /device:TPU:0, one launch (start us, length us, event | category | flops | bytes accessed | tf_op | source)
XLA Modules:
  0.0 1443.7 jit_solution(14899728928498230009)
XLA Ops:
  0.7 8.8 bitcast_convert_fusion.1
  50.8 12.0 fusion.65
  73.2 5.3 convolution_bitcast_fusion.95
  79.0 5.6 fusion.53
  188.9 15.0 %fusion.1088 = (bf16[3,512,1024]{2,1,0:T(8,128)(2,1)}, f32[3,512,1024]{2,1,0:T(8,128)}) fusion(f32[1,512,1024]{2,1,0:T(8,128)} %convolution_bitcast_fusion.87, f32[1,512,1024]{2,1,0:T(8,128)} %convolution_bitcast_fusion.88, f32[1,512,1024]{2,1,0:T(8,128)} %convolution_bitcast_fusion.89, f32[1,512,1024]{2,1,0:T(8,128)} %convolution_bitcast_fusion.93, ...), kind=kLoop, calls=%fused_computation.1703 | loop fusion | flops 25165824 | bytes 37748736 | tf_op jit(solution)/shard_map/convert_element_type | solution.py:70
  207.5 8.0 fusion.1086
  251.7 5.8 convolution_bitcast_fusion.83
  257.5 5.6 subtract_convert_fusion.13
  278.2 36.7 %collective-permute-done.5 = bf16[3,512,1024]{2,1,0:T(8,128)(2,1)} collective-permute-done((bf16[3,512,1024]{2,1,0:T(8,128)(2,1)}, bf16[3,512,1024]{2,1,0:T(8,128)(2,1)}, u32[]{:S(2)}, u32[]{:S(2)}) %collective-permute-start.5) | collective-permute-done | bytes 3145760 | tf_op jit(solution)/shard_map/ppermute | solution.py:73
  330.5 15.0 %fusion.1084 = (bf16[3,512,1024]{2,1,0:T(8,128)(2,1)}, f32[3,512,1024]{2,1,0:T(8,128)}) fusion(f32[1,512,1024]{2,1,0:T(8,128)} %convolution_bitcast_fusion.75, f32[1,512,1024]{2,1,0:T(8,128)} %convolution_bitcast_fusion.76, f32[1,512,1024]{2,1,0:T(8,128)} %convolution_bitcast_fusion.77, f32[1,512,1024]{2,1,0:T(8,128)} %convolution_bitcast_fusion.81, ...), kind=kLoop, calls=%fused_computation.1701 | loop fusion | flops 25165824 | bytes 37748736 | tf_op jit(solution)/shard_map/convert_element_type | solution.py:70
  348.9 31.4 %collective-permute-done.14 = bf16[3,1024,512]{2,1,0:T(8,128)(2,1)} collective-permute-done((bf16[3,1024,512]{2,1,0:T(8,128)(2,1)}, bf16[3,1024,512]{2,1,0:T(8,128)(2,1)}, u32[]{:S(2)}, u32[]{:S(2)}) %collective-permute-start.14) | collective-permute-done | bytes 3145760 | tf_op jit(solution)/shard_map/ppermute | solution.py:73
  383.3 8.2 fusion.1082
  426.0 5.8 convolution_bitcast_fusion.71
  431.9 5.6 subtract_convert_fusion.11
  452.1 38.9 %collective-permute-done.11 = bf16[3,512,1024]{2,1,0:T(8,128)(2,1)} collective-permute-done((bf16[3,512,1024]{2,1,0:T(8,128)(2,1)}, bf16[3,512,1024]{2,1,0:T(8,128)(2,1)}, u32[]{:S(2)}, u32[]{:S(2)}) %collective-permute-start.11) | collective-permute-done | bytes 3145760 | tf_op jit(solution)/shard_map/ppermute | solution.py:73
  506.6 15.0 %fusion.1080 = (bf16[3,512,1024]{2,1,0:T(8,128)(2,1)}, f32[3,512,1024]{2,1,0:T(8,128)}) fusion(f32[1,512,1024]{2,1,0:T(8,128)} %convolution_bitcast_fusion.63, f32[1,512,1024]{2,1,0:T(8,128)} %convolution_bitcast_fusion.64, f32[1,512,1024]{2,1,0:T(8,128)} %convolution_bitcast_fusion.65, f32[1,512,1024]{2,1,0:T(8,128)} %convolution_bitcast_fusion.69, ...), kind=kLoop, calls=%fused_computation.1699 | loop fusion | flops 25165824 | bytes 37748736 | tf_op jit(solution)/shard_map/convert_element_type | solution.py:70
  525.2 30.0 %collective-permute-done.20 = bf16[3,1024,512]{2,1,0:T(8,128)(2,1)} collective-permute-done((bf16[3,1024,512]{2,1,0:T(8,128)(2,1)}, bf16[3,1024,512]{2,1,0:T(8,128)(2,1)}, u32[]{:S(2)}, u32[]{:S(2)}) %collective-permute-start.20) | collective-permute-done | bytes 3145760 | tf_op jit(solution)/shard_map/ppermute | solution.py:73
  558.3 8.2 fusion.1078
  600.5 5.8 convolution_bitcast_fusion.59
  606.4 5.6 subtract_convert_fusion.9
  626.6 39.4 %collective-permute-done.17 = bf16[3,512,1024]{2,1,0:T(8,128)(2,1)} collective-permute-done((bf16[3,512,1024]{2,1,0:T(8,128)(2,1)}, bf16[3,512,1024]{2,1,0:T(8,128)(2,1)}, u32[]{:S(2)}, u32[]{:S(2)}) %collective-permute-start.17) | collective-permute-done | bytes 3145760 | tf_op jit(solution)/shard_map/ppermute | solution.py:73
  681.7 15.0 %fusion.1076 = (bf16[3,512,1024]{2,1,0:T(8,128)(2,1)}, f32[3,512,1024]{2,1,0:T(8,128)}) fusion(f32[1,512,1024]{2,1,0:T(8,128)} %convolution_bitcast_fusion.51, f32[1,512,1024]{2,1,0:T(8,128)} %convolution_bitcast_fusion.52, f32[1,512,1024]{2,1,0:T(8,128)} %convolution_bitcast_fusion.53, f32[1,512,1024]{2,1,0:T(8,128)} %convolution_bitcast_fusion.57, ...), kind=kLoop, calls=%fused_computation.1697 | loop fusion | flops 25165824 | bytes 37748736 | tf_op jit(solution)/shard_map/convert_element_type | solution.py:70
  700.3 30.3 %collective-permute-done.26 = bf16[3,1024,512]{2,1,0:T(8,128)(2,1)} collective-permute-done((bf16[3,1024,512]{2,1,0:T(8,128)(2,1)}, bf16[3,1024,512]{2,1,0:T(8,128)(2,1)}, u32[]{:S(2)}, u32[]{:S(2)}) %collective-permute-start.26) | collective-permute-done | bytes 3145760 | tf_op jit(solution)/shard_map/ppermute | solution.py:73
  734.2 8.2 fusion.1074
  776.4 5.8 convolution_bitcast_fusion.47
  782.2 5.6 subtract_convert_fusion.7
  802.4 39.4 %collective-permute-done.23 = bf16[3,512,1024]{2,1,0:T(8,128)(2,1)} collective-permute-done((bf16[3,512,1024]{2,1,0:T(8,128)(2,1)}, bf16[3,512,1024]{2,1,0:T(8,128)(2,1)}, u32[]{:S(2)}, u32[]{:S(2)}) %collective-permute-start.23) | collective-permute-done | bytes 3145760 | tf_op jit(solution)/shard_map/ppermute | solution.py:73
  857.5 15.0 %fusion.1072 = (bf16[3,512,1024]{2,1,0:T(8,128)(2,1)}, f32[3,512,1024]{2,1,0:T(8,128)}) fusion(f32[1,512,1024]{2,1,0:T(8,128)} %convolution_bitcast_fusion.39, f32[1,512,1024]{2,1,0:T(8,128)} %convolution_bitcast_fusion.40, f32[1,512,1024]{2,1,0:T(8,128)} %convolution_bitcast_fusion.41, f32[1,512,1024]{2,1,0:T(8,128)} %convolution_bitcast_fusion.45, ...), kind=kLoop, calls=%fused_computation.1695 | loop fusion | flops 25165824 | bytes 37748736 | tf_op jit(solution)/shard_map/convert_element_type | solution.py:70
  876.1 30.4 %collective-permute-done.32 = bf16[3,1024,512]{2,1,0:T(8,128)(2,1)} collective-permute-done((bf16[3,1024,512]{2,1,0:T(8,128)(2,1)}, bf16[3,1024,512]{2,1,0:T(8,128)(2,1)}, u32[]{:S(2)}, u32[]{:S(2)}) %collective-permute-start.32) | collective-permute-done | bytes 3145760 | tf_op jit(solution)/shard_map/ppermute | solution.py:73
  909.4 8.2 fusion.1070
  951.6 5.8 convolution_bitcast_fusion.35
  957.5 5.6 subtract_convert_fusion.5
  977.7 39.4 %collective-permute-done.29 = bf16[3,512,1024]{2,1,0:T(8,128)(2,1)} collective-permute-done((bf16[3,512,1024]{2,1,0:T(8,128)(2,1)}, bf16[3,512,1024]{2,1,0:T(8,128)(2,1)}, u32[]{:S(2)}, u32[]{:S(2)}) %collective-permute-start.29) | collective-permute-done | bytes 3145760 | tf_op jit(solution)/shard_map/ppermute | solution.py:73
  1032.7 15.0 %fusion.1068 = (bf16[3,512,1024]{2,1,0:T(8,128)(2,1)}, f32[3,512,1024]{2,1,0:T(8,128)}) fusion(f32[1,512,1024]{2,1,0:T(8,128)} %convolution_bitcast_fusion.27, f32[1,512,1024]{2,1,0:T(8,128)} %convolution_bitcast_fusion.28, f32[1,512,1024]{2,1,0:T(8,128)} %convolution_bitcast_fusion.29, f32[1,512,1024]{2,1,0:T(8,128)} %convolution_bitcast_fusion.33, ...), kind=kLoop, calls=%fused_computation.1693 | loop fusion | flops 25165824 | bytes 37748736 | tf_op jit(solution)/shard_map/convert_element_type | solution.py:70
  1051.2 30.5 %collective-permute-done.38 = bf16[3,1024,512]{2,1,0:T(8,128)(2,1)} collective-permute-done((bf16[3,1024,512]{2,1,0:T(8,128)(2,1)}, bf16[3,1024,512]{2,1,0:T(8,128)(2,1)}, u32[]{:S(2)}, u32[]{:S(2)}) %collective-permute-start.38) | collective-permute-done | bytes 3145760 | tf_op jit(solution)/shard_map/ppermute | solution.py:73
  1084.5 8.2 fusion.1066
  1126.7 5.8 convolution_bitcast_fusion.23
  1132.6 5.6 subtract_convert_fusion.3
  1152.8 39.4 %collective-permute-done.35 = bf16[3,512,1024]{2,1,0:T(8,128)(2,1)} collective-permute-done((bf16[3,512,1024]{2,1,0:T(8,128)(2,1)}, bf16[3,512,1024]{2,1,0:T(8,128)(2,1)}, u32[]{:S(2)}, u32[]{:S(2)}) %collective-permute-start.35) | collective-permute-done | bytes 3145760 | tf_op jit(solution)/shard_map/ppermute | solution.py:73
  1207.8 14.9 %fusion.1064 = (bf16[3,512,1024]{2,1,0:T(8,128)(2,1)}, f32[3,512,1024]{2,1,0:T(8,128)}) fusion(f32[1,512,1024]{2,1,0:T(8,128)} %convolution_bitcast_fusion.15, f32[1,512,1024]{2,1,0:T(8,128)} %convolution_bitcast_fusion.16, f32[1,512,1024]{2,1,0:T(8,128)} %convolution_bitcast_fusion.17, f32[1,512,1024]{2,1,0:T(8,128)} %convolution_bitcast_fusion.21, ...), kind=kLoop, calls=%fused_computation.1691 | loop fusion | flops 25165824 | bytes 37748736 | tf_op jit(solution)/shard_map/convert_element_type | solution.py:70
  1226.3 30.5 %collective-permute-done.44 = bf16[3,1024,512]{2,1,0:T(8,128)(2,1)} collective-permute-done((bf16[3,1024,512]{2,1,0:T(8,128)(2,1)}, bf16[3,1024,512]{2,1,0:T(8,128)(2,1)}, u32[]{:S(2)}, u32[]{:S(2)}) %collective-permute-start.44) | collective-permute-done | bytes 3145760 | tf_op jit(solution)/shard_map/ppermute | solution.py:73
  1259.8 8.4 fusion.1062
  1302.3 5.8 convolution_bitcast_fusion.11
  1308.1 5.6 subtract_convert_fusion.1
  1327.9 39.8 %collective-permute-done.41 = bf16[3,512,1024]{2,1,0:T(8,128)(2,1)} collective-permute-done((bf16[3,512,1024]{2,1,0:T(8,128)(2,1)}, bf16[3,512,1024]{2,1,0:T(8,128)(2,1)}, u32[]{:S(2)}, u32[]{:S(2)}) %collective-permute-start.41) | collective-permute-done | bytes 3145760 | tf_op jit(solution)/shard_map/ppermute | solution.py:73
  1383.7 13.8 fusion.28
  1397.6 34.8 %collective-permute-done.47 = bf16[3,1024,512]{2,1,0:T(8,128)(2,1)} collective-permute-done((bf16[3,1024,512]{2,1,0:T(8,128)(2,1)}, bf16[3,1024,512]{2,1,0:T(8,128)(2,1)}, u32[]{:S(2)}, u32[]{:S(2)}) %collective-permute-start.47) | collective-permute-done | bytes 3145760 | tf_op jit(solution)/shard_map/ppermute | solution.py:73
  1436.0 7.6 fusion.33
  (922 shorter events, 653.0 us)
Async XLA Ops:
  9.5 140.8 %collective-permute-start.2 = (bf16[3,512,1024]{2,1,0:T(8,128)(2,1)}, bf16[3,512,1024]{2,1,0:T(8,128)(2,1)}, u32[]{:S(2)}, u32[]{:S(2)}) collective-permute-start(bf16[3,512,1024]{2,1,0:T(8,128)(2,1)} %get-tuple-element.64), channel_id=1, source_target_pairs={{0,8},{8,0},{1,9},{9,1},{2,10},{10,2},{3,11},{11,3},{4,12},{12,4},... | collective-permute-start | bytes 9437192 | tf_op jit(solution)/shard_map/ppermute | solution.py:73
  12.8 176.0 %collective-permute-start.1 = (bf16[3,512,1024]{2,1,0:T(8,128)(2,1)}, bf16[3,512,1024]{2,1,0:T(8,128)(2,1)}, u32[]{:S(2)}, u32[]{:S(2)}) collective-permute-start(bf16[3,512,1024]{2,1,0:T(8,128)(2,1)} %get-tuple-element.64), channel_id=1, source_target_pairs={{0,7},{1,0},{2,1},{3,2},{4,3},{5,4},{6,5},{7,6},{8,15},{9,8},{10,9... | collective-permute-start | bytes 9437192 | tf_op jit(solution)/shard_map/ppermute | solution.py:73
  14.4 174.4 %collective-permute-start = (bf16[3,512,1024]{2,1,0:T(8,128)(2,1)}, bf16[3,512,1024]{2,1,0:T(8,128)(2,1)}, u32[]{:S(2)}, u32[]{:S(2)}) collective-permute-start(bf16[3,512,1024]{2,1,0:T(8,128)(2,1)} %get-tuple-element.64), channel_id=1, source_target_pairs={{0,1},{1,2},{2,3},{3,4},{4,5},{5,6},{6,7},{7,0},{8,9},{9,10},{10,1... | collective-permute-start | bytes 9437192 | tf_op jit(solution)/shard_map/ppermute | solution.py:73
  16.6 190.8 %collective-permute-start.8 = (bf16[3,1024,512]{2,1,0:T(8,128)(2,1)}, bf16[3,1024,512]{2,1,0:T(8,128)(2,1)}, u32[]{:S(2)}, u32[]{:S(2)}) collective-permute-start(bf16[3,1024,512]{2,1,0:T(8,128)(2,1)} %get-tuple-element.62), channel_id=1, source_target_pairs={{0,8},{8,0},{1,9},{9,1},{2,10},{10,2},{3,11},{11,3},{4,12},{12,4},... | collective-permute-start | bytes 9437192 | tf_op jit(solution)/shard_map/ppermute | solution.py:73
  17.1 190.3 %collective-permute-start.7 = (bf16[3,1024,512]{2,1,0:T(8,128)(2,1)}, bf16[3,1024,512]{2,1,0:T(8,128)(2,1)}, u32[]{:S(2)}, u32[]{:S(2)}) collective-permute-start(bf16[3,1024,512]{2,1,0:T(8,128)(2,1)} %get-tuple-element.62), channel_id=1, source_target_pairs={{0,7},{1,0},{2,1},{3,2},{4,3},{5,4},{6,5},{7,6},{8,15},{9,8},{10,9... | collective-permute-start | bytes 9437192 | tf_op jit(solution)/shard_map/ppermute | solution.py:73
  150.3 57.1 %collective-permute-start.6 = (bf16[3,1024,512]{2,1,0:T(8,128)(2,1)}, bf16[3,1024,512]{2,1,0:T(8,128)(2,1)}, u32[]{:S(2)}, u32[]{:S(2)}) collective-permute-start(bf16[3,1024,512]{2,1,0:T(8,128)(2,1)} %get-tuple-element.62), channel_id=1, source_target_pairs={{0,1},{1,2},{2,3},{3,4},{4,5},{5,6},{6,7},{7,0},{8,9},{9,10},{10,1... | collective-permute-start | bytes 9437192 | tf_op jit(solution)/shard_map/ppermute | solution.py:73
  243.9 71.0 %collective-permute-start.5 = (bf16[3,512,1024]{2,1,0:T(8,128)(2,1)}, bf16[3,512,1024]{2,1,0:T(8,128)(2,1)}, u32[]{:S(2)}, u32[]{:S(2)}) collective-permute-start(bf16[3,512,1024]{2,1,0:T(8,128)(2,1)} %get-tuple-element.28), channel_id=1, source_target_pairs={{0,8},{8,0},{1,9},{9,1},{2,10},{10,2},{3,11},{11,3},{4,12},{12,4},... | collective-permute-start | bytes 9437192 | tf_op jit(solution)/shard_map/ppermute | solution.py:73
  245.4 85.0 %collective-permute-start.4 = (bf16[3,512,1024]{2,1,0:T(8,128)(2,1)}, bf16[3,512,1024]{2,1,0:T(8,128)(2,1)}, u32[]{:S(2)}, u32[]{:S(2)}) collective-permute-start(bf16[3,512,1024]{2,1,0:T(8,128)(2,1)} %get-tuple-element.28), channel_id=1, source_target_pairs={{0,7},{1,0},{2,1},{3,2},{4,3},{5,4},{6,5},{7,6},{8,15},{9,8},{10,9... | collective-permute-start | bytes 9437192 | tf_op jit(solution)/shard_map/ppermute | solution.py:73
  247.8 82.6 %collective-permute-start.3 = (bf16[3,512,1024]{2,1,0:T(8,128)(2,1)}, bf16[3,512,1024]{2,1,0:T(8,128)(2,1)}, u32[]{:S(2)}, u32[]{:S(2)}) collective-permute-start(bf16[3,512,1024]{2,1,0:T(8,128)(2,1)} %get-tuple-element.28), channel_id=1, source_target_pairs={{0,1},{1,2},{2,3},{3,4},{4,5},{5,6},{6,7},{7,0},{8,9},{9,10},{10,1... | collective-permute-start | bytes 9437192 | tf_op jit(solution)/shard_map/ppermute | solution.py:73
  247.8 132.6 %collective-permute-start.14 = (bf16[3,1024,512]{2,1,0:T(8,128)(2,1)}, bf16[3,1024,512]{2,1,0:T(8,128)(2,1)}, u32[]{:S(2)}, u32[]{:S(2)}) collective-permute-start(bf16[3,1024,512]{2,1,0:T(8,128)(2,1)} %get-tuple-element.26), channel_id=1, source_target_pairs={{0,8},{8,0},{1,9},{9,1},{2,10},{10,2},{3,11},{11,3},{4,12},{12,4},... | collective-permute-start | bytes 9437192 | tf_op jit(solution)/shard_map/ppermute | solution.py:73
  248.2 132.9 %collective-permute-start.13 = (bf16[3,1024,512]{2,1,0:T(8,128)(2,1)}, bf16[3,1024,512]{2,1,0:T(8,128)(2,1)}, u32[]{:S(2)}, u32[]{:S(2)}) collective-permute-start(bf16[3,1024,512]{2,1,0:T(8,128)(2,1)} %get-tuple-element.26), channel_id=1, source_target_pairs={{0,7},{1,0},{2,1},{3,2},{4,3},{5,4},{6,5},{7,6},{8,15},{9,8},{10,9... | collective-permute-start | bytes 9437192 | tf_op jit(solution)/shard_map/ppermute | solution.py:73
  314.8 68.4 %collective-permute-start.12 = (bf16[3,1024,512]{2,1,0:T(8,128)(2,1)}, bf16[3,1024,512]{2,1,0:T(8,128)(2,1)}, u32[]{:S(2)}, u32[]{:S(2)}) collective-permute-start(bf16[3,1024,512]{2,1,0:T(8,128)(2,1)} %get-tuple-element.26), channel_id=1, source_target_pairs={{0,1},{1,2},{2,3},{3,4},{4,5},{5,6},{6,7},{7,0},{8,9},{9,10},{10,1... | collective-permute-start | bytes 9437192 | tf_op jit(solution)/shard_map/ppermute | solution.py:73
  420.0 71.0 %collective-permute-start.11 = (bf16[3,512,1024]{2,1,0:T(8,128)(2,1)}, bf16[3,512,1024]{2,1,0:T(8,128)(2,1)}, u32[]{:S(2)}, u32[]{:S(2)}) collective-permute-start(bf16[3,512,1024]{2,1,0:T(8,128)(2,1)} %get-tuple-element.24), channel_id=1, source_target_pairs={{0,8},{8,0},{1,9},{9,1},{2,10},{10,2},{3,11},{11,3},{4,12},{12,4},... | collective-permute-start | bytes 9437192 | tf_op jit(solution)/shard_map/ppermute | solution.py:73
  420.5 86.1 %collective-permute-start.10 = (bf16[3,512,1024]{2,1,0:T(8,128)(2,1)}, bf16[3,512,1024]{2,1,0:T(8,128)(2,1)}, u32[]{:S(2)}, u32[]{:S(2)}) collective-permute-start(bf16[3,512,1024]{2,1,0:T(8,128)(2,1)} %get-tuple-element.24), channel_id=1, source_target_pairs={{0,7},{1,0},{2,1},{3,2},{4,3},{5,4},{6,5},{7,6},{8,15},{9,8},{10,9... | collective-permute-start | bytes 9437192 | tf_op jit(solution)/shard_map/ppermute | solution.py:73
  420.8 85.7 %collective-permute-start.9 = (bf16[3,512,1024]{2,1,0:T(8,128)(2,1)}, bf16[3,512,1024]{2,1,0:T(8,128)(2,1)}, u32[]{:S(2)}, u32[]{:S(2)}) collective-permute-start(bf16[3,512,1024]{2,1,0:T(8,128)(2,1)} %get-tuple-element.24), channel_id=1, source_target_pairs={{0,1},{1,2},{2,3},{3,4},{4,5},{5,6},{6,7},{7,0},{8,9},{9,10},{10,1... | collective-permute-start | bytes 9437192 | tf_op jit(solution)/shard_map/ppermute | solution.py:73
  421.0 134.2 %collective-permute-start.20 = (bf16[3,1024,512]{2,1,0:T(8,128)(2,1)}, bf16[3,1024,512]{2,1,0:T(8,128)(2,1)}, u32[]{:S(2)}, u32[]{:S(2)}) collective-permute-start(bf16[3,1024,512]{2,1,0:T(8,128)(2,1)} %get-tuple-element.22), channel_id=1, source_target_pairs={{0,8},{8,0},{1,9},{9,1},{2,10},{10,2},{3,11},{11,3},{4,12},{12,4},... | collective-permute-start | bytes 9437192 | tf_op jit(solution)/shard_map/ppermute | solution.py:73
  422.6 132.6 %collective-permute-start.19 = (bf16[3,1024,512]{2,1,0:T(8,128)(2,1)}, bf16[3,1024,512]{2,1,0:T(8,128)(2,1)}, u32[]{:S(2)}, u32[]{:S(2)}) collective-permute-start(bf16[3,1024,512]{2,1,0:T(8,128)(2,1)} %get-tuple-element.22), channel_id=1, source_target_pairs={{0,7},{1,0},{2,1},{3,2},{4,3},{5,4},{6,5},{7,6},{8,15},{9,8},{10,9... | collective-permute-start | bytes 9437192 | tf_op jit(solution)/shard_map/ppermute | solution.py:73
  491.0 67.3 %collective-permute-start.18 = (bf16[3,1024,512]{2,1,0:T(8,128)(2,1)}, bf16[3,1024,512]{2,1,0:T(8,128)(2,1)}, u32[]{:S(2)}, u32[]{:S(2)}) collective-permute-start(bf16[3,1024,512]{2,1,0:T(8,128)(2,1)} %get-tuple-element.22), channel_id=1, source_target_pairs={{0,1},{1,2},{2,3},{3,4},{4,5},{5,6},{6,7},{7,0},{8,9},{9,10},{10,1... | collective-permute-start | bytes 9437192 | tf_op jit(solution)/shard_map/ppermute | solution.py:73
  595.0 71.0 %collective-permute-start.17 = (bf16[3,512,1024]{2,1,0:T(8,128)(2,1)}, bf16[3,512,1024]{2,1,0:T(8,128)(2,1)}, u32[]{:S(2)}, u32[]{:S(2)}) collective-permute-start(bf16[3,512,1024]{2,1,0:T(8,128)(2,1)} %get-tuple-element.20), channel_id=1, source_target_pairs={{0,8},{8,0},{1,9},{9,1},{2,10},{10,2},{3,11},{11,3},{4,12},{12,4},... | collective-permute-start | bytes 9437192 | tf_op jit(solution)/shard_map/ppermute | solution.py:73
  596.3 85.3 %collective-permute-start.16 = (bf16[3,512,1024]{2,1,0:T(8,128)(2,1)}, bf16[3,512,1024]{2,1,0:T(8,128)(2,1)}, u32[]{:S(2)}, u32[]{:S(2)}) collective-permute-start(bf16[3,512,1024]{2,1,0:T(8,128)(2,1)} %get-tuple-element.20), channel_id=1, source_target_pairs={{0,7},{1,0},{2,1},{3,2},{4,3},{5,4},{6,5},{7,6},{8,15},{9,8},{10,9... | collective-permute-start | bytes 9437192 | tf_op jit(solution)/shard_map/ppermute | solution.py:73
  596.3 85.3 %collective-permute-start.15 = (bf16[3,512,1024]{2,1,0:T(8,128)(2,1)}, bf16[3,512,1024]{2,1,0:T(8,128)(2,1)}, u32[]{:S(2)}, u32[]{:S(2)}) collective-permute-start(bf16[3,512,1024]{2,1,0:T(8,128)(2,1)} %get-tuple-element.20), channel_id=1, source_target_pairs={{0,1},{1,2},{2,3},{3,4},{4,5},{5,6},{6,7},{7,0},{8,9},{9,10},{10,1... | collective-permute-start | bytes 9437192 | tf_op jit(solution)/shard_map/ppermute | solution.py:73
  596.8 133.7 %collective-permute-start.26 = (bf16[3,1024,512]{2,1,0:T(8,128)(2,1)}, bf16[3,1024,512]{2,1,0:T(8,128)(2,1)}, u32[]{:S(2)}, u32[]{:S(2)}) collective-permute-start(bf16[3,1024,512]{2,1,0:T(8,128)(2,1)} %get-tuple-element.18), channel_id=1, source_target_pairs={{0,8},{8,0},{1,9},{9,1},{2,10},{10,2},{3,11},{11,3},{4,12},{12,4},... | collective-permute-start | bytes 9437192 | tf_op jit(solution)/shard_map/ppermute | solution.py:73
  597.6 133.0 %collective-permute-start.25 = (bf16[3,1024,512]{2,1,0:T(8,128)(2,1)}, bf16[3,1024,512]{2,1,0:T(8,128)(2,1)}, u32[]{:S(2)}, u32[]{:S(2)}) collective-permute-start(bf16[3,1024,512]{2,1,0:T(8,128)(2,1)} %get-tuple-element.18), channel_id=1, source_target_pairs={{0,7},{1,0},{2,1},{3,2},{4,3},{5,4},{6,5},{7,6},{8,15},{9,8},{10,9... | collective-permute-start | bytes 9437192 | tf_op jit(solution)/shard_map/ppermute | solution.py:73
  666.0 68.1 %collective-permute-start.24 = (bf16[3,1024,512]{2,1,0:T(8,128)(2,1)}, bf16[3,1024,512]{2,1,0:T(8,128)(2,1)}, u32[]{:S(2)}, u32[]{:S(2)}) collective-permute-start(bf16[3,1024,512]{2,1,0:T(8,128)(2,1)} %get-tuple-element.18), channel_id=1, source_target_pairs={{0,1},{1,2},{2,3},{3,4},{4,5},{5,6},{6,7},{7,0},{8,9},{9,10},{10,1... | collective-permute-start | bytes 9437192 | tf_op jit(solution)/shard_map/ppermute | solution.py:73
  770.9 71.0 %collective-permute-start.23 = (bf16[3,512,1024]{2,1,0:T(8,128)(2,1)}, bf16[3,512,1024]{2,1,0:T(8,128)(2,1)}, u32[]{:S(2)}, u32[]{:S(2)}) collective-permute-start(bf16[3,512,1024]{2,1,0:T(8,128)(2,1)} %get-tuple-element.16), channel_id=1, source_target_pairs={{0,8},{8,0},{1,9},{9,1},{2,10},{10,2},{3,11},{11,3},{4,12},{12,4},... | collective-permute-start | bytes 9437192 | tf_op jit(solution)/shard_map/ppermute | solution.py:73
  771.7 85.8 %collective-permute-start.22 = (bf16[3,512,1024]{2,1,0:T(8,128)(2,1)}, bf16[3,512,1024]{2,1,0:T(8,128)(2,1)}, u32[]{:S(2)}, u32[]{:S(2)}) collective-permute-start(bf16[3,512,1024]{2,1,0:T(8,128)(2,1)} %get-tuple-element.16), channel_id=1, source_target_pairs={{0,7},{1,0},{2,1},{3,2},{4,3},{5,4},{6,5},{7,6},{8,15},{9,8},{10,9... | collective-permute-start | bytes 9437192 | tf_op jit(solution)/shard_map/ppermute | solution.py:73
  771.7 85.8 %collective-permute-start.21 = (bf16[3,512,1024]{2,1,0:T(8,128)(2,1)}, bf16[3,512,1024]{2,1,0:T(8,128)(2,1)}, u32[]{:S(2)}, u32[]{:S(2)}) collective-permute-start(bf16[3,512,1024]{2,1,0:T(8,128)(2,1)} %get-tuple-element.16), channel_id=1, source_target_pairs={{0,1},{1,2},{2,3},{3,4},{4,5},{5,6},{6,7},{7,0},{8,9},{9,10},{10,1... | collective-permute-start | bytes 9437192 | tf_op jit(solution)/shard_map/ppermute | solution.py:73
  772.2 134.3 %collective-permute-start.32 = (bf16[3,1024,512]{2,1,0:T(8,128)(2,1)}, bf16[3,1024,512]{2,1,0:T(8,128)(2,1)}, u32[]{:S(2)}, u32[]{:S(2)}) collective-permute-start(bf16[3,1024,512]{2,1,0:T(8,128)(2,1)} %get-tuple-element.14), channel_id=1, source_target_pairs={{0,8},{8,0},{1,9},{9,1},{2,10},{10,2},{3,11},{11,3},{4,12},{12,4},... | collective-permute-start | bytes 9437192 | tf_op jit(solution)/shard_map/ppermute | solution.py:73
  773.4 133.1 %collective-permute-start.31 = (bf16[3,1024,512]{2,1,0:T(8,128)(2,1)}, bf16[3,1024,512]{2,1,0:T(8,128)(2,1)}, u32[]{:S(2)}, u32[]{:S(2)}) collective-permute-start(bf16[3,1024,512]{2,1,0:T(8,128)(2,1)} %get-tuple-element.14), channel_id=1, source_target_pairs={{0,7},{1,0},{2,1},{3,2},{4,3},{5,4},{6,5},{7,6},{8,15},{9,8},{10,9... | collective-permute-start | bytes 9437192 | tf_op jit(solution)/shard_map/ppermute | solution.py:73
  841.9 67.5 %collective-permute-start.30 = (bf16[3,1024,512]{2,1,0:T(8,128)(2,1)}, bf16[3,1024,512]{2,1,0:T(8,128)(2,1)}, u32[]{:S(2)}, u32[]{:S(2)}) collective-permute-start(bf16[3,1024,512]{2,1,0:T(8,128)(2,1)} %get-tuple-element.14), channel_id=1, source_target_pairs={{0,1},{1,2},{2,3},{3,4},{4,5},{5,6},{6,7},{7,0},{8,9},{9,10},{10,1... | collective-permute-start | bytes 9437192 | tf_op jit(solution)/shard_map/ppermute | solution.py:73
  946.1 71.0 %collective-permute-start.29 = (bf16[3,512,1024]{2,1,0:T(8,128)(2,1)}, bf16[3,512,1024]{2,1,0:T(8,128)(2,1)}, u32[]{:S(2)}, u32[]{:S(2)}) collective-permute-start(bf16[3,512,1024]{2,1,0:T(8,128)(2,1)} %get-tuple-element.12), channel_id=1, source_target_pairs={{0,8},{8,0},{1,9},{9,1},{2,10},{10,2},{3,11},{11,3},{4,12},{12,4},... | collective-permute-start | bytes 9437192 | tf_op jit(solution)/shard_map/ppermute | solution.py:73
  946.6 86.1 %collective-permute-start.28 = (bf16[3,512,1024]{2,1,0:T(8,128)(2,1)}, bf16[3,512,1024]{2,1,0:T(8,128)(2,1)}, u32[]{:S(2)}, u32[]{:S(2)}) collective-permute-start(bf16[3,512,1024]{2,1,0:T(8,128)(2,1)} %get-tuple-element.12), channel_id=1, source_target_pairs={{0,7},{1,0},{2,1},{3,2},{4,3},{5,4},{6,5},{7,6},{8,15},{9,8},{10,9... | collective-permute-start | bytes 9437192 | tf_op jit(solution)/shard_map/ppermute | solution.py:73
  946.6 86.1 %collective-permute-start.27 = (bf16[3,512,1024]{2,1,0:T(8,128)(2,1)}, bf16[3,512,1024]{2,1,0:T(8,128)(2,1)}, u32[]{:S(2)}, u32[]{:S(2)}) collective-permute-start(bf16[3,512,1024]{2,1,0:T(8,128)(2,1)} %get-tuple-element.12), channel_id=1, source_target_pairs={{0,1},{1,2},{2,3},{3,4},{4,5},{5,6},{6,7},{7,0},{8,9},{9,10},{10,1... | collective-permute-start | bytes 9437192 | tf_op jit(solution)/shard_map/ppermute | solution.py:73
  947.1 134.7 %collective-permute-start.38 = (bf16[3,1024,512]{2,1,0:T(8,128)(2,1)}, bf16[3,1024,512]{2,1,0:T(8,128)(2,1)}, u32[]{:S(2)}, u32[]{:S(2)}) collective-permute-start(bf16[3,1024,512]{2,1,0:T(8,128)(2,1)} %get-tuple-element.10), channel_id=1, source_target_pairs={{0,8},{8,0},{1,9},{9,1},{2,10},{10,2},{3,11},{11,3},{4,12},{12,4},... | collective-permute-start | bytes 9437192 | tf_op jit(solution)/shard_map/ppermute | solution.py:73
  948.7 133.1 %collective-permute-start.37 = (bf16[3,1024,512]{2,1,0:T(8,128)(2,1)}, bf16[3,1024,512]{2,1,0:T(8,128)(2,1)}, u32[]{:S(2)}, u32[]{:S(2)}) collective-permute-start(bf16[3,1024,512]{2,1,0:T(8,128)(2,1)} %get-tuple-element.10), channel_id=1, source_target_pairs={{0,7},{1,0},{2,1},{3,2},{4,3},{5,4},{6,5},{7,6},{8,15},{9,8},{10,9... | collective-permute-start | bytes 9437192 | tf_op jit(solution)/shard_map/ppermute | solution.py:73
  1017.1 67.3 %collective-permute-start.36 = (bf16[3,1024,512]{2,1,0:T(8,128)(2,1)}, bf16[3,1024,512]{2,1,0:T(8,128)(2,1)}, u32[]{:S(2)}, u32[]{:S(2)}) collective-permute-start(bf16[3,1024,512]{2,1,0:T(8,128)(2,1)} %get-tuple-element.10), channel_id=1, source_target_pairs={{0,1},{1,2},{2,3},{3,4},{4,5},{5,6},{6,7},{7,0},{8,9},{9,10},{10,1... | collective-permute-start | bytes 9437192 | tf_op jit(solution)/shard_map/ppermute | solution.py:73
  1121.2 71.0 %collective-permute-start.35 = (bf16[3,512,1024]{2,1,0:T(8,128)(2,1)}, bf16[3,512,1024]{2,1,0:T(8,128)(2,1)}, u32[]{:S(2)}, u32[]{:S(2)}) collective-permute-start(bf16[3,512,1024]{2,1,0:T(8,128)(2,1)} %get-tuple-element.8), channel_id=1, source_target_pairs={{0,8},{8,0},{1,9},{9,1},{2,10},{10,2},{3,11},{11,3},{4,12},{12,4},... | collective-permute-start | bytes 9437192 | tf_op jit(solution)/shard_map/ppermute | solution.py:73
  1122.0 85.8 %collective-permute-start.34 = (bf16[3,512,1024]{2,1,0:T(8,128)(2,1)}, bf16[3,512,1024]{2,1,0:T(8,128)(2,1)}, u32[]{:S(2)}, u32[]{:S(2)}) collective-permute-start(bf16[3,512,1024]{2,1,0:T(8,128)(2,1)} %get-tuple-element.8), channel_id=1, source_target_pairs={{0,7},{1,0},{2,1},{3,2},{4,3},{5,4},{6,5},{7,6},{8,15},{9,8},{10,9... | collective-permute-start | bytes 9437192 | tf_op jit(solution)/shard_map/ppermute | solution.py:73
  1122.0 85.8 %collective-permute-start.33 = (bf16[3,512,1024]{2,1,0:T(8,128)(2,1)}, bf16[3,512,1024]{2,1,0:T(8,128)(2,1)}, u32[]{:S(2)}, u32[]{:S(2)}) collective-permute-start(bf16[3,512,1024]{2,1,0:T(8,128)(2,1)} %get-tuple-element.8), channel_id=1, source_target_pairs={{0,1},{1,2},{2,3},{3,4},{4,5},{5,6},{6,7},{7,0},{8,9},{9,10},{10,1... | collective-permute-start | bytes 9437192 | tf_op jit(solution)/shard_map/ppermute | solution.py:73
  1122.5 134.3 %collective-permute-start.44 = (bf16[3,1024,512]{2,1,0:T(8,128)(2,1)}, bf16[3,1024,512]{2,1,0:T(8,128)(2,1)}, u32[]{:S(2)}, u32[]{:S(2)}) collective-permute-start(bf16[3,1024,512]{2,1,0:T(8,128)(2,1)} %get-tuple-element.6), channel_id=1, source_target_pairs={{0,8},{8,0},{1,9},{9,1},{2,10},{10,2},{3,11},{11,3},{4,12},{12,4},... | collective-permute-start | bytes 9437192 | tf_op jit(solution)/shard_map/ppermute | solution.py:73
  1123.8 133.0 %collective-permute-start.43 = (bf16[3,1024,512]{2,1,0:T(8,128)(2,1)}, bf16[3,1024,512]{2,1,0:T(8,128)(2,1)}, u32[]{:S(2)}, u32[]{:S(2)}) collective-permute-start(bf16[3,1024,512]{2,1,0:T(8,128)(2,1)} %get-tuple-element.6), channel_id=1, source_target_pairs={{0,7},{1,0},{2,1},{3,2},{4,3},{5,4},{6,5},{7,6},{8,15},{9,8},{10,9... | collective-permute-start | bytes 9437192 | tf_op jit(solution)/shard_map/ppermute | solution.py:73
  1192.2 67.6 %collective-permute-start.42 = (bf16[3,1024,512]{2,1,0:T(8,128)(2,1)}, bf16[3,1024,512]{2,1,0:T(8,128)(2,1)}, u32[]{:S(2)}, u32[]{:S(2)}) collective-permute-start(bf16[3,1024,512]{2,1,0:T(8,128)(2,1)} %get-tuple-element.6), channel_id=1, source_target_pairs={{0,1},{1,2},{2,3},{3,4},{4,5},{5,6},{6,7},{7,0},{8,9},{9,10},{10,1... | collective-permute-start | bytes 9437192 | tf_op jit(solution)/shard_map/ppermute | solution.py:73
  1296.8 71.0 %collective-permute-start.41 = (bf16[3,512,1024]{2,1,0:T(8,128)(2,1)}, bf16[3,512,1024]{2,1,0:T(8,128)(2,1)}, u32[]{:S(2)}, u32[]{:S(2)}) collective-permute-start(bf16[3,512,1024]{2,1,0:T(8,128)(2,1)} %get-tuple-element.4), channel_id=1, source_target_pairs={{0,8},{8,0},{1,9},{9,1},{2,10},{10,2},{3,11},{11,3},{4,12},{12,4},... | collective-permute-start | bytes 9437192 | tf_op jit(solution)/shard_map/ppermute | solution.py:73
  1298.1 85.6 %collective-permute-start.40 = (bf16[3,512,1024]{2,1,0:T(8,128)(2,1)}, bf16[3,512,1024]{2,1,0:T(8,128)(2,1)}, u32[]{:S(2)}, u32[]{:S(2)}) collective-permute-start(bf16[3,512,1024]{2,1,0:T(8,128)(2,1)} %get-tuple-element.4), channel_id=1, source_target_pairs={{0,7},{1,0},{2,1},{3,2},{4,3},{5,4},{6,5},{7,6},{8,15},{9,8},{10,9... | collective-permute-start | bytes 9437192 | tf_op jit(solution)/shard_map/ppermute | solution.py:73
  1298.1 85.7 %collective-permute-start.39 = (bf16[3,512,1024]{2,1,0:T(8,128)(2,1)}, bf16[3,512,1024]{2,1,0:T(8,128)(2,1)}, u32[]{:S(2)}, u32[]{:S(2)}) collective-permute-start(bf16[3,512,1024]{2,1,0:T(8,128)(2,1)} %get-tuple-element.4), channel_id=1, source_target_pairs={{0,1},{1,2},{2,3},{3,4},{4,5},{5,6},{6,7},{7,0},{8,9},{9,10},{10,1... | collective-permute-start | bytes 9437192 | tf_op jit(solution)/shard_map/ppermute | solution.py:73
  1298.6 133.8 %collective-permute-start.47 = (bf16[3,1024,512]{2,1,0:T(8,128)(2,1)}, bf16[3,1024,512]{2,1,0:T(8,128)(2,1)}, u32[]{:S(2)}, u32[]{:S(2)}) collective-permute-start(bf16[3,1024,512]{2,1,0:T(8,128)(2,1)} %get-tuple-element.2), channel_id=1, source_target_pairs={{0,8},{8,0},{1,9},{9,1},{2,10},{10,2},{3,11},{11,3},{4,12},{12,4},... | collective-permute-start | bytes 9437192 | tf_op jit(solution)/shard_map/ppermute | solution.py:73
  1299.3 133.1 %collective-permute-start.46 = (bf16[3,1024,512]{2,1,0:T(8,128)(2,1)}, bf16[3,1024,512]{2,1,0:T(8,128)(2,1)}, u32[]{:S(2)}, u32[]{:S(2)}) collective-permute-start(bf16[3,1024,512]{2,1,0:T(8,128)(2,1)} %get-tuple-element.2), channel_id=1, source_target_pairs={{0,7},{1,0},{2,1},{3,2},{4,3},{5,4},{6,5},{7,6},{8,15},{9,8},{10,9... | collective-permute-start | bytes 9437192 | tf_op jit(solution)/shard_map/ppermute | solution.py:73
  1367.7 68.2 %collective-permute-start.45 = (bf16[3,1024,512]{2,1,0:T(8,128)(2,1)}, bf16[3,1024,512]{2,1,0:T(8,128)(2,1)}, u32[]{:S(2)}, u32[]{:S(2)}) collective-permute-start(bf16[3,1024,512]{2,1,0:T(8,128)(2,1)} %get-tuple-element.2), channel_id=1, source_target_pairs={{0,1},{1,2},{2,3},{3,4},{4,5},{5,6},{6,7},{7,0},{8,9},{9,10},{10,1... | collective-permute-start | bytes 9437192 | tf_op jit(solution)/shard_map/ppermute | solution.py:73
  (202 other events, 3478.8 us)
where the time goes:
time: 1460 us; the launch traced here: 1440 us
  matrix products  528 us (36%)
  waiting for transfers between devices  513 us (35%)
  other arithmetic  288 us (20%)
  local copies, waits for them, and re-layouts  69.2 us (5%)
  starting transfers between devices  41.4 us (3%)
    ppermute x48, waiting for transfers between devices, neighbour_mix(): lax.ppermute(wire_copy, axis_name, pair_list).astype(jnp.float32)  513 us
    dot_general x48, matrix products, device_grads(): lax.dot_general(normed, d_pre, CONTRACT_ROWS, preferred_element_type=jnp....  155 us
    another operation x23, other arithmetic  116 us
    convert_element_type x9, other arithmetic, neighbour_mix(): wire_copy = params.astype(jnp.bfloat16)  116 us
    dot_general x48, matrix products, device_grads(): pre_act = jnp.dot(normed, w1_bf, preferred_element_type=jnp.float32)  97.4 us
    dot_general x48, matrix products, device_grads(): lax.dot_general(act_bf, grad_bf, CONTRACT_ROWS, preferred_element_type=jn...  91.1 us
    dot_general x32, matrix products, device_grads(): lax.dot_general(grad_bf, w2_bf, CONTRACT_LAST, preferred_element_type=jnp...  76.8 us
    dot_general x48, matrix products, device_grads(): jnp.dot(act_bf, w2_bf, preferred_element_type=jnp.float32)  65.5 us
  transfers between devices with their start and end apart: 48, of which 22 were waited for; matrix products, arithmetic and copies ran while one was open for 41% of the time, Pallas kernels for 0%

commit v1 on v0

v1 whole, which is shorter than its diff:
```python
import jax
import jax.numpy as jnp
from jax import lax
from jax.experimental import pallas as pl
from jax.experimental.pallas import tpu as pltpu
from jax.sharding import PartitionSpec as P

LR_SCALE = 0.8
EPS = 1e-6
INV_SQRT2 = 0.7071067811865476
INV_SQRT_2PI = 0.3989422804014327
CONTRACT_ROWS = (((0,), (0,)), ((), ()))
CONTRACT_LAST = (((1,), (1,)), ((), ()))
MESH = pl.DeviceIdType.MESH
F32 = jnp.float32
BF16 = jnp.bfloat16

PARTS = 4
ROW_BLOCK = 256


def solution(mesh):
    col_size = mesh.shape["col"]

    def device_kernel(w1_hbm, w2_hbm, a_hbm, t_hbm, out1, out2, got1, got2,
                      p1, p2, sum1, sum2, pb1, pb2, qb1, qb2,
                      hid, normed, slope, act, grad_h, grad_bf, d_pre, rows_buf, tgt_buf, stage1, stage2,
                      load_sem, data_sem, stage_sem, send_sem, recv_sem):
        layers, dim, ff = p1.shape
        batch = rows_buf.shape[1]
        steps = a_hbm.shape[0]
        windows = steps // 2
        learn_rate = LR_SCALE / layers
        rows1, rows2 = dim // PARTS, ff // PARTS
        pieces = layers * PARTS

        row = lax.axis_index("row")
        col = lax.axis_index("col")
        targets = [(row, lax.rem(col + 1, col_size)), (row, lax.rem(col + col_size - 1, col_size)), (1 - row, col)]

        def piece(idx):
            layer = idx // PARTS
            part = lax.rem(idx, PARTS)
            at1 = (layer, pl.ds(pl.multiple_of(part * rows1, rows1), rows1))
            at2 = (layer, pl.ds(pl.multiple_of(part * rows2, rows2), rows2))
            return at1, at2

        def sends(idx, slot):
            at1, at2 = piece(idx)
            copies = []
            for k, target in enumerate(targets):
                for which, (src, dst, at) in enumerate(((pb1, got1, at1), (pb2, got2, at2))):
                    copies.append(pltpu.make_async_remote_copy(
                        src_ref=src.at[at], dst_ref=dst.at[(slot, k) + at],
                        send_sem=send_sem.at[idx, which, k], recv_sem=recv_sem.at[slot, idx, which, k],
                        device_id=target, device_id_type=MESH))
            return copies

        def loads(idx):
            at1, at2 = piece(idx)
            return [pltpu.make_async_copy(w1_hbm.at[at1], p1.at[at1], load_sem.at[idx, 0]),
                    pltpu.make_async_copy(w2_hbm.at[at2], p2.at[at2], load_sem.at[idx, 1])]

        def stores(idx):
            at1, at2 = piece(idx)
            return [pltpu.make_async_copy(p1.at[at1], out1.at[at1], load_sem.at[idx, 0]),
                    pltpu.make_async_copy(p2.at[at2], out2.at[at2], load_sem.at[idx, 1])]

        def fetch(step):
            slot = lax.rem(step, 2)
            return [pltpu.make_async_copy(a_hbm.at[step], rows_buf.at[slot], data_sem.at[slot, 0]),
                    pltpu.make_async_copy(t_hbm.at[step], tgt_buf.at[slot], data_sem.at[slot, 1])]

        def start_all(copies):
            for copy in copies:
                copy.start()

        def wait_all(copies):
            for copy in copies:
                copy.wait()

        def load_one(idx, carry):
            start_all(loads(idx))
            return carry
        lax.fori_loop(0, pieces, load_one, 0)
        start_all(fetch(0))

        barrier = pltpu.get_barrier_semaphore()
        for target in targets:
            pl.semaphore_signal(barrier, inc=1, device_id=target, device_id_type=MESH)
        pl.semaphore_wait(barrier, len(targets))

        def first_send(idx, carry):
            wait_all(loads(idx))
            at1, at2 = piece(idx)
            pb1[at1] = p1[at1].astype(BF16)
            pb2[at2] = p2[at2].astype(BF16)
            start_all(sends(idx, 0))
            return carry
        lax.fori_loop(0, pieces, first_send, 0)

        def local_step(step, first, wb1, wb2):
            slot = 0 if first else 1
            wait_all(fetch(step))
            @pl.when(step + 1 < steps)
            def _():
                start_all(fetch(step + 1))

            def rms_rows(src, layer):
                def body(i, carry):
                    at = pl.ds(pl.multiple_of(i * 32, 32), 32)
                    v = src[at].astype(F32)
                    normed[layer, at] = (v * lax.rsqrt(jnp.mean(v * v, axis=-1, keepdims=True) + EPS)).astype(BF16)
                    return carry
                lax.fori_loop(0, batch // 32, body, 0)

            def forward(layer, h_in, h_out):
                rms_rows(h_in, layer)
                for blk in range(batch // ROW_BLOCK):
                    rows = pl.ds(blk * ROW_BLOCK, ROW_BLOCK)
                    slope[layer, rows] = jnp.dot(normed[layer, rows], wb1[layer], preferred_element_type=F32)

                    def gelu(i, carry):
                        at = pl.ds(pl.multiple_of(blk * ROW_BLOCK + i * 16, 16), 16)
                        for half in range(2):
                            lanes = pl.ds(half * (ff // 2), ff // 2)
                            z = slope[layer, at, lanes]
                            phi = 0.5 * (1.0 + lax.erf(z * INV_SQRT2))
                            act[layer, at, lanes] = (z * phi).astype(BF16)
                            slope[layer, at, lanes] = phi + z * jnp.exp(-0.5 * z * z) * INV_SQRT_2PI
                        return carry
                    lax.fori_loop(0, ROW_BLOCK // 16, gelu, 0)
                    h_out[rows] = (h_in[rows].astype(F32) + jnp.dot(act[layer, rows], wb2[layer], preferred_element_type=F32)).astype(BF16)

            forward(0, rows_buf.at[slot], hid.at[0])

            def forward_rest(layer, carry):
                forward(layer, hid.at[layer - 1], hid.at[layer])
                return carry
            lax.fori_loop(1, layers, forward_rest, 0)

            def loss(i, carry):
                at = pl.ds(pl.multiple_of(i * 32, 32), 32)
                e = (hid[layers - 1, at].astype(F32) - tgt_buf[slot, at].astype(F32)) * (2.0 / (batch * dim))
                grad_h[at] = e
                grad_bf[at] = e.astype(BF16)
                return carry
            lax.fori_loop(0, batch // 32, loss, 0)

            def apply(p, total, qb, layer, at, grad):
                if first:
                    total[layer, at] = grad
                    qb[layer, at] = (p[layer, at] - learn_rate * grad).astype(BF16)
                else:
                    total[layer, at] = learn_rate * (total[layer, at] + grad)

            def backward(back, carry):
                layer = layers - 1 - back
                for tile in range(ff // 256):
                    at = pl.ds(tile * 256, 256)
                    apply(p2, sum2, qb2, layer, at,
                          lax.dot_general(act[layer, :, at], grad_bf[...], CONTRACT_ROWS, preferred_element_type=F32))
                for blk in range(batch // ROW_BLOCK):
                    rows = pl.ds(blk * ROW_BLOCK, ROW_BLOCK)
                    d_pre[rows] = (lax.dot_general(grad_bf[rows], wb2[layer], CONTRACT_LAST, preferred_element_type=F32)
                                   * slope[layer, rows]).astype(BF16)
                for tile in range(dim // 128):
                    at = pl.ds(tile * 128, 128)
                    apply(p1, sum1, qb1, layer, at,
                          lax.dot_general(normed[layer, :, at], d_pre[...], CONTRACT_ROWS, preferred_element_type=F32))

                @pl.when(layer > 0)
                def _():
                    h_in = hid.at[layer - 1]
                    for blk in range(batch // ROW_BLOCK):
                        rows = pl.ds(blk * ROW_BLOCK, ROW_BLOCK)
                        grad_norm = lax.dot_general(d_pre[rows], wb1[layer], CONTRACT_LAST, preferred_element_type=F32)
                        h = h_in[rows].astype(F32)
                        inv_rms = lax.rsqrt(jnp.mean(h * h, axis=-1, keepdims=True) + EPS)
                        row_dot = jnp.mean(h * grad_norm, axis=-1, keepdims=True)
                        e = grad_h[rows] + (inv_rms * grad_norm - h * (inv_rms * inv_rms * inv_rms) * row_dot)
                        grad_h[rows] = e
                        grad_bf[rows] = e.astype(BF16)
                return carry
            lax.fori_loop(0, layers, backward, 0)

        def mix(window):
            slot = lax.rem(window, 2)

            def one(idx, carry):
                at1, at2 = piece(idx)
                wait_all(sends(idx, slot))
                staged = []
                for k in range(len(targets)):
                    staged.append(pltpu.make_async_copy(got1.at[(slot, k) + at1], stage1.at[k], stage_sem.at[0, k]))
                    staged.append(pltpu.make_async_copy(got2.at[(slot, k) + at2], stage2.at[k], stage_sem.at[1, k]))
                start_all(staged)
                wait_all(staged)
                for p, pb, total, stage, (layer, span) in ((p1, pb1, sum1, stage1, at1), (p2, pb2, sum2, stage2, at2)):
                    rows = stage.shape[1]
                    base = lax.rem(idx, PARTS) * rows

                    def some(i, inner):
                        src = pl.ds(pl.multiple_of(i * 16, 16), 16)
                        at = (layer, pl.ds(pl.multiple_of(base + i * 16, 16), 16))
                        acc = p[at] + stage[0, src].astype(F32)
                        acc = acc + stage[1, src].astype(F32)
                        other = stage[2, src].astype(F32)
                        acc = (acc + other) + other
                        new = acc / 5.0 - total[at]
                        p[at] = new
                        pb[at] = new.astype(BF16)
                        return inner
                    lax.fori_loop(0, rows // 16, some, 0)

                @pl.when(window + 1 < windows)
                def _():
                    start_all(sends(idx, 1 - slot))

                @pl.when(window + 1 == windows)
                def _():
                    start_all(stores(idx))
                return carry
            lax.fori_loop(0, pieces, one, 0)

        def one_window(window, carry):
            local_step(2 * window, True, pb1, pb2)
            local_step(2 * window + 1, False, qb1, qb2)
            mix(window)
            return carry
        lax.fori_loop(0, windows, one_window, 0)

        def finish(idx, carry):
            wait_all(stores(idx))
            return carry
        lax.fori_loop(0, pieces, finish, 0)

    def device_program(w_in, w_out, inputs, targets):
        layers, dim, ff = w_in.shape[2:]
        steps, batch = inputs.shape[2:4]
        pieces = layers * PARTS
        any_space = pl.BlockSpec(memory_space=pl.ANY)
        shape1, shape2 = (layers, dim, ff), (layers, ff, dim)
        sums = pl.pallas_call(
            device_kernel,
            out_shape=[jax.ShapeDtypeStruct(shape1, F32), jax.ShapeDtypeStruct(shape2, F32),
                       jax.ShapeDtypeStruct((2, 3) + shape1, BF16), jax.ShapeDtypeStruct((2, 3) + shape2, BF16)],
            in_specs=[any_space] * 4,
            out_specs=[any_space] * 4,
            scratch_shapes=[
                pltpu.VMEM(shape1, F32), pltpu.VMEM(shape2, F32),
                pltpu.VMEM(shape1, F32), pltpu.VMEM(shape2, F32),
                pltpu.VMEM(shape1, BF16), pltpu.VMEM(shape2, BF16),
                pltpu.VMEM(shape1, BF16), pltpu.VMEM(shape2, BF16),
                pltpu.VMEM((layers, batch, dim), BF16),
                pltpu.VMEM((layers, batch, dim), BF16),
                pltpu.VMEM((layers, batch, ff), F32),
                pltpu.VMEM((layers, batch, ff), BF16),
                pltpu.VMEM((batch, dim), F32),
                pltpu.VMEM((batch, dim), BF16),
                pltpu.VMEM((batch, ff), BF16),
                pltpu.VMEM((2, batch, dim), BF16), pltpu.VMEM((2, batch, dim), BF16),
                pltpu.VMEM((3, dim // PARTS, ff), BF16), pltpu.VMEM((3, ff // PARTS, dim), BF16),
                pltpu.SemaphoreType.DMA((pieces, 2)),
                pltpu.SemaphoreType.DMA((2, 2)),
                pltpu.SemaphoreType.DMA((2, 3)),
                pltpu.SemaphoreType.DMA((pieces, 2, 3)),
                pltpu.SemaphoreType.DMA((2, pieces, 2, 3)),
            ],
            compiler_params=pltpu.CompilerParams(collective_id=0, has_side_effects=True, vmem_limit_bytes=67043328),
        )(w_in[0, 0], w_out[0, 0], inputs[0, 0], targets[0, 0])
        return sums[0][None, None], sums[1][None, None]

    block_spec = P("row", "col")
    return jax.shard_map(device_program, mesh=mesh,
                         in_specs=(block_spec, block_spec, block_spec, block_spec),
                         out_specs=(block_spec, block_spec), check_vma=False)
```

time: 1460 us -> 1100 us (0.75); the launches traced: 1440 us -> 1100 us
  Pallas kernels: 0 us -> 1090 us
  matrix products: 528 us -> 0 us
  waiting for transfers between devices: 513 us -> 0 us
  other arithmetic: 288 us -> 0 us
  local copies, waits for them, and re-layouts: 69.2 us -> 9.47 us
  starting transfers between devices: 41.4 us -> 0 us
    pallas_call x0 -> x1, Pallas kernels: none -> 1090 us  [device_program(): pl.pallas_call(device_kernel, out_shape=[jax.ShapeDtypeStruct(shape1, F32...]
    dot_general x256 -> x0, matrix products: 528 us -> none  [the longest x48 155 us: device_grads(): lax.dot_general(normed, d_pre, CONTRACT_ROWS, preferred_element_type=jnp....]
    ppermute x48 -> x0, waiting for transfers between devices: 513 us -> none  [neighbour_mix(): lax.ppermute(wire_copy, axis_name, pair_list).astype(jnp.float32)]
    convert_element_type x25 -> x0, other arithmetic: 123 us -> none  [the longest x9 116 us: neighbour_mix(): wire_copy = params.astype(jnp.bfloat16)]
    another operation x23 -> x0, other arithmetic: 116 us -> none
    unnamed x436 -> x4, local copies, waits for them, and re-layouts: 62.4 us -> 9.47 us
    ppermute x48 -> x0, starting transfers between devices: 41.4 us -> none  [neighbour_mix(): lax.ppermute(wire_copy, axis_name, pair_list).astype(jnp.float32)]
    broadcast_in_dim x2 -> x0, other arithmetic: 21.4 us -> none  [device_program(): return (cur_in[None, None], cur_out[None, None])]
  transfers between devices with their start and end apart: 48 -> 0, of which waited for: 22 -> 0; matrix products, arithmetic and copies ran while one was open for 41% -> 0% of each run, Pallas kernels for 0% -> 0%
where the time goes in v1:
time: 1100 us
  Pallas kernels  1090 us (99%)
    pallas_call x1, Pallas kernels, device_program(): pl.pallas_call(device_kernel, out_shape=[jax.ShapeDtypeStruct(shape1, F32...  1090 us

profile of v1, /device:TPU:0, one launch (start us, length us, event | category | flops | bytes accessed | tf_op | source)
XLA Modules:
  0.0 1099.8 jit_solution(1185744623956653755)
XLA Ops:
  0.6 1089.7 %shard_map.59 = (f32[3,512,1024]{2,1,0:T(8,128)}, f32[3,1024,512]{2,1,0:T(8,128)}, bf16[2,3,3,512,1024]{4,3,2,1,0:T(8,128)(2,1)}, bf16[2,3,3,1024,512]{4,3,2,1,0:T(8,128)(2,1)}) custom-call(f32[3,512,1024]{2,1,0:T(8,128)} %bitcast.8, f32[3,1024,512]{2,1,0:T(8,128)} %bitcast.9, bf16[16,512,512]{2,1,0:T(8,128)(2,1)} %bitcast.6, bf16[16,512,512]{2,1,0:T(8,128)(2,1)} %bitcast.7), custom_call_target="tpu_custom_call" | custom-call | tf_op jit(solution)/shard_map/pallas_call | solution.py:244
  1090.3 0.0 copy-start
  1090.4 6.8 copy.8
  1097.1 0.0 copy-done
  1097.1 2.7 copy.9
Async XLA Ops:
  1090.3 6.8 copy-start

commit v2 on v1

--- a/solution.py
+++ b/solution.py
@@ -15,15 +15,15 @@
 F32 = jnp.float32
 BF16 = jnp.bfloat16
 
-PARTS = 4
+PARTS = 2
 ROW_BLOCK = 256
 
 
 def solution(mesh):
     col_size = mesh.shape["col"]
 
-    def device_kernel(w1_hbm, w2_hbm, a_hbm, t_hbm, out1, out2, got1, got2,
-                      p1, p2, sum1, sum2, pb1, pb2, qb1, qb2,
+    def device_kernel(w1_hbm, w2_hbm, a_hbm, t_hbm, p1, p2, got1, got2,
+                      sum1, sum2, pb1, pb2, qb1, qb2,
                       hid, normed, slope, act, grad_h, grad_bf, d_pre, rows_buf, tgt_buf, stage1, stage2,
                       load_sem, data_sem, stage_sem, send_sem, recv_sem):
         layers, dim, ff = p1.shape
@@ -45,27 +45,19 @@
             at2 = (layer, pl.ds(pl.multiple_of(part * rows2, rows2), rows2))
             return at1, at2
 
-        def sends(idx, slot):
-            at1, at2 = piece(idx)
-            copies = []
-            for k, target in enumerate(targets):
-                for which, (src, dst, at) in enumerate(((pb1, got1, at1), (pb2, got2, at2))):
-                    copies.append(pltpu.make_async_remote_copy(
-                        src_ref=src.at[at], dst_ref=dst.at[(slot, k) + at],
-                        send_sem=send_sem.at[idx, which, k], recv_sem=recv_sem.at[slot, idx, which, k],
-                        device_id=target, device_id_type=MESH))
-            return copies
+        def sends(idx, slot, which):
+            src, dst = ((pb1, got1), (pb2, got2))[which]
+            at = piece(idx)[which]
+            return [pltpu.make_async_remote_copy(
+                src_ref=src.at[at], dst_ref=dst.at[(slot, k) + at],
+                send_sem=send_sem.at[idx, which, k], recv_sem=recv_sem.at[slot, idx, which, k],
+                device_id=target, device_id_type=MESH) for k, target in enumerate(targets)]
 
         def loads(idx):
             at1, at2 = piece(idx)
             return [pltpu.make_async_copy(w1_hbm.at[at1], p1.at[at1], load_sem.at[idx, 0]),
                     pltpu.make_async_copy(w2_hbm.at[at2], p2.at[at2], load_sem.at[idx, 1])]
 
-        def stores(idx):
-            at1, at2 = piece(idx)
-            return [pltpu.make_async_copy(p1.at[at1], out1.at[at1], load_sem.at[idx, 0]),
-                    pltpu.make_async_copy(p2.at[at2], out2.at[at2], load_sem.at[idx, 1])]
-
         def fetch(step):
             slot = lax.rem(step, 2)
             return [pltpu.make_async_copy(a_hbm.at[step], rows_buf.at[slot], data_sem.at[slot, 0]),
@@ -79,11 +71,9 @@
             for copy in copies:
                 copy.wait()
 
-        def load_one(idx, carry):
+        ahead = min(3, pieces)
+        for idx in range(ahead):
             start_all(loads(idx))
-            return carry
-        lax.fori_loop(0, pieces, load_one, 0)
-        start_all(fetch(0))
 
         barrier = pltpu.get_barrier_semaphore()
         for target in targets:
@@ -91,13 +81,18 @@
         pl.semaphore_wait(barrier, len(targets))
 
         def first_send(idx, carry):
-            wait_all(loads(idx))
-            at1, at2 = piece(idx)
-            pb1[at1] = p1[at1].astype(BF16)
-            pb2[at2] = p2[at2].astype(BF16)
-            start_all(sends(idx, 0))
+            for which, (load, p, pb) in enumerate(zip(loads(idx), (p1, p2), (pb1, pb2))):
+                load.wait()
+                at = piece(idx)[which]
+                pb[at] = p[at].astype(BF16)
+                start_all(sends(idx, 0, which))
+
+            @pl.when(idx + ahead < pieces)
+            def _():
+                start_all(loads(idx + ahead))
             return carry
         lax.fori_loop(0, pieces, first_send, 0)
+        start_all(fetch(0))
 
         def local_step(step, first, wb1, wb2):
             slot = 0 if first else 1
@@ -188,15 +183,14 @@
             slot = lax.rem(window, 2)
 
             def one(idx, carry):
-                at1, at2 = piece(idx)
-                wait_all(sends(idx, slot))
-                staged = []
-                for k in range(len(targets)):
-                    staged.append(pltpu.make_async_copy(got1.at[(slot, k) + at1], stage1.at[k], stage_sem.at[0, k]))
-                    staged.append(pltpu.make_async_copy(got2.at[(slot, k) + at2], stage2.at[k], stage_sem.at[1, k]))
-                start_all(staged)
-                wait_all(staged)
-                for p, pb, total, stage, (layer, span) in ((p1, pb1, sum1, stage1, at1), (p2, pb2, sum2, stage2, at2)):
+                for which, (p, pb, total, got, stage) in enumerate(
+                        ((p1, pb1, sum1, got1, stage1), (p2, pb2, sum2, got2, stage2))):
+                    wait_all(sends(idx, slot, which))
+                    layer, span = at_piece = piece(idx)[which]
+                    staged = [pltpu.make_async_copy(got.at[(slot, k) + at_piece], stage.at[k], stage_sem.at[which, k])
+                              for k in range(len(targets))]
+                    start_all(staged)
+                    wait_all(staged)
                     rows = stage.shape[1]
                     base = lax.rem(idx, PARTS) * rows
 
@@ -213,13 +207,9 @@
                         return inner
                     lax.fori_loop(0, rows // 16, some, 0)
 
-                @pl.when(window + 1 < windows)
-                def _():
-                    start_all(sends(idx, 1 - slot))
-
-                @pl.when(window + 1 == windows)
-                def _():
-                    start_all(stores(idx))
+                    @pl.when(window + 1 < windows)
+                    def _():
+                        start_all(sends(idx, 1 - slot, which))
                 return carry
             lax.fori_loop(0, pieces, one, 0)
 
@@ -229,11 +219,6 @@
             mix(window)
             return carry
         lax.fori_loop(0, windows, one_window, 0)
-
-        def finish(idx, carry):
-            wait_all(stores(idx))
-            return carry
-        lax.fori_loop(0, pieces, finish, 0)
 
     def device_program(w_in, w_out, inputs, targets):
         layers, dim, ff = w_in.shape[2:]
@@ -243,12 +228,11 @@
         shape1, shape2 = (layers, dim, ff), (layers, ff, dim)
         sums = pl.pallas_call(
             device_kernel,
-            out_shape=[jax.ShapeDtypeStruct(shape1, F32), jax.ShapeDtypeStruct(shape2, F32),
+            out_shape=[pltpu.VMEM(shape1, F32), pltpu.VMEM(shape2, F32),
                        jax.ShapeDtypeStruct((2, 3) + shape1, BF16), jax.ShapeDtypeStruct((2, 3) + shape2, BF16)],
             in_specs=[any_space] * 4,
-            out_specs=[any_space] * 4,
+            out_specs=[pl.BlockSpec(memory_space=pltpu.VMEM)] * 2 + [any_space] * 2,
             scratch_shapes=[
-                pltpu.VMEM(shape1, F32), pltpu.VMEM(shape2, F32),
                 pltpu.VMEM(shape1, F32), pltpu.VMEM(shape2, F32),
                 pltpu.VMEM(shape1, BF16), pltpu.VMEM(shape2, BF16),
                 pltpu.VMEM(shape1, BF16), pltpu.VMEM(shape2, BF16),
@@ -267,7 +251,7 @@
                 pltpu.SemaphoreType.DMA((pieces, 2, 3)),
                 pltpu.SemaphoreType.DMA((2, pieces, 2, 3)),
             ],
-            compiler_params=pltpu.CompilerParams(collective_id=0, has_side_effects=True, vmem_limit_bytes=67043328),
+            compiler_params=pltpu.CompilerParams(collective_id=0, has_side_effects=True, vmem_limit_bytes=52_000_000),
         )(w_in[0, 0], w_out[0, 0], inputs[0, 0], targets[0, 0])
         return sums[0][None, None], sums[1][None, None]
 

time: 1100 us -> 1100 us (level)
  no operation moved by 1% of the time
where the time goes in v2:
time: 1100 us; the launch traced here: 1090 us
  Pallas kernels  1090 us (99%)
    pallas_call x1, Pallas kernels, device_program(): pl.pallas_call(device_kernel, out_shape=[pltpu.VMEM(shape1, F32), pltpu.V...  1090 us

profile of v2, /device:TPU:0, one launch (start us, length us, event | category | flops | bytes accessed | tf_op | source)
XLA Modules:
  0.0 1093.6 jit_solution(16255694868395731808)
XLA Ops:
  0.6 1087.6 %shard_map.59 = (f32[3,512,1024]{2,1,0:T(8,128)S(1)}, f32[3,1024,512]{2,1,0:T(8,128)S(1)}, bf16[2,3,3,512,1024]{4,3,2,1,0:T(8,128)(2,1)}, bf16[2,3,3,1024,512]{4,3,2,1,0:T(8,128)(2,1)}) custom-call(f32[3,512,1024]{2,1,0:T(8,128)} %bitcast.10, f32[3,1024,512]{2,1,0:T(8,128)} %bitcast.11, bf16[16,512,512]{2,1,0:T(8,128)(2,1)} %bitcast.8, ...), custom_call_target="tpu_custom_call" | custom-call | tf_op jit(solution)/shard_map/pallas_call | solution.py:229
  1088.2 2.7 copy.8
  1090.9 2.7 copy.9

commit v3 on v2

--- a/solution.py
+++ b/solution.py
@@ -15,8 +15,24 @@
 F32 = jnp.float32
 BF16 = jnp.bfloat16
 
-PARTS = 2
+FIRST_ROWS = (64, 192)
+LAST_ROWS = (256, 128)
 ROW_BLOCK = 256
+
+
+def exchange_table(layers, dim, ff):
+    table, start = [], 0
+    for part in FIRST_ROWS + (dim - sum(FIRST_ROWS),):
+        table.append((0, 0, start, part))
+        start += part
+    table.append((1, 0, 0, ff))
+    for layer in range(1, layers):
+        table += [(0, layer, 0, dim), (1, layer, 0, ff)]
+    which, layer, start, rows = table.pop()
+    for part in (rows - sum(LAST_ROWS),) + LAST_ROWS:
+        table.append((which, layer, start, part))
+        start += part
+    return table
 
 
 def solution(mesh):
@@ -24,39 +40,40 @@
 
     def device_kernel(w1_hbm, w2_hbm, a_hbm, t_hbm, p1, p2, got1, got2,
                       sum1, sum2, pb1, pb2, qb1, qb2,
-                      hid, normed, slope, act, grad_h, grad_bf, d_pre, rows_buf, tgt_buf, stage1, stage2,
+                      hid, normed, slope, act, grad_h, grad_bf, d_pre, rows_buf, tgt_buf, stage1, stage2, tail,
                       load_sem, data_sem, stage_sem, send_sem, recv_sem):
         layers, dim, ff = p1.shape
         batch = rows_buf.shape[1]
         steps = a_hbm.shape[0]
         windows = steps // 2
         learn_rate = LR_SCALE / layers
-        rows1, rows2 = dim // PARTS, ff // PARTS
-        pieces = layers * PARTS
+        params, bf_params, totals = (p1, p2), (pb1, pb2), (sum1, sum2)
+        table = exchange_table(layers, dim, ff)
 
         row = lax.axis_index("row")
         col = lax.axis_index("col")
         targets = [(row, lax.rem(col + 1, col_size)), (row, lax.rem(col + col_size - 1, col_size)), (1 - row, col)]
 
-        def piece(idx):
-            layer = idx // PARTS
-            part = lax.rem(idx, PARTS)
-            at1 = (layer, pl.ds(pl.multiple_of(part * rows1, rows1), rows1))
-            at2 = (layer, pl.ds(pl.multiple_of(part * rows2, rows2), rows2))
-            return at1, at2
-
-        def sends(idx, slot, which):
-            src, dst = ((pb1, got1), (pb2, got2))[which]
-            at = piece(idx)[which]
+        def span(idx):
+            _, layer, start, rows = table[idx]
+            return layer, pl.ds(start, rows)
+
+        def landing(idx, slot, k):
+            which, _, _, _ = table[idx]
+            if idx == len(table) - 1:
+                return tail.at[slot, k]
+            return (got1, got2)[which].at[(slot, k) + span(idx)]
+
+        def sends(idx, slot):
+            src = bf_params[table[idx][0]].at[span(idx)]
             return [pltpu.make_async_remote_copy(
-                src_ref=src.at[at], dst_ref=dst.at[(slot, k) + at],
-                send_sem=send_sem.at[idx, which, k], recv_sem=recv_sem.at[slot, idx, which, k],
+                src_ref=src, dst_ref=landing(idx, slot, k),
+                send_sem=send_sem.at[idx, k], recv_sem=recv_sem.at[slot, idx, k],
                 device_id=target, device_id_type=MESH) for k, target in enumerate(targets)]
 
-        def loads(idx):
-            at1, at2 = piece(idx)
-            return [pltpu.make_async_copy(w1_hbm.at[at1], p1.at[at1], load_sem.at[idx, 0]),
-                    pltpu.make_async_copy(w2_hbm.at[at2], p2.at[at2], load_sem.at[idx, 1])]
+        def load(idx):
+            which = table[idx][0]
+            return pltpu.make_async_copy((w1_hbm, w2_hbm)[which].at[span(idx)], params[which].at[span(idx)], load_sem.at[idx])
 
         def fetch(step):
             slot = lax.rem(step, 2)
@@ -71,27 +88,26 @@
             for copy in copies:
                 copy.wait()
 
-        ahead = min(3, pieces)
-        for idx in range(ahead):
-            start_all(loads(idx))
+        load(0).start()
 
         barrier = pltpu.get_barrier_semaphore()
         for target in targets:
             pl.semaphore_signal(barrier, inc=1, device_id=target, device_id_type=MESH)
         pl.semaphore_wait(barrier, len(targets))
 
-        def first_send(idx, carry):
-            for which, (load, p, pb) in enumerate(zip(loads(idx), (p1, p2), (pb1, pb2))):
-                load.wait()
-                at = piece(idx)[which]
+        for idx, (which, layer, start, rows) in enumerate(table):
+            if idx == 0:
+                for later in range(1, len(table)):
+                    load(later).start()
+            load(idx).wait()
+            p, pb = params[which], bf_params[which]
+
+            def cast(i, carry):
+                at = (layer, pl.ds(pl.multiple_of(start + i * 32, 32), 32))
                 pb[at] = p[at].astype(BF16)
-                start_all(sends(idx, 0, which))
-
-            @pl.when(idx + ahead < pieces)
-            def _():
-                start_all(loads(idx + ahead))
-            return carry
-        lax.fori_loop(0, pieces, first_send, 0)
+                return carry
+            lax.fori_loop(0, rows // 32, cast, 0)
+            start_all(sends(idx, 0))
         start_all(fetch(0))
 
         def local_step(step, first, wb1, wb2):
@@ -182,36 +198,34 @@
         def mix(window):
             slot = lax.rem(window, 2)
 
-            def one(idx, carry):
-                for which, (p, pb, total, got, stage) in enumerate(
-                        ((p1, pb1, sum1, got1, stage1), (p2, pb2, sum2, got2, stage2))):
-                    wait_all(sends(idx, slot, which))
-                    layer, span = at_piece = piece(idx)[which]
-                    staged = [pltpu.make_async_copy(got.at[(slot, k) + at_piece], stage.at[k], stage_sem.at[which, k])
+            for idx, (which, layer, start, rows) in enumerate(table):
+                p, pb, total = params[which], bf_params[which], totals[which]
+                wait_all(sends(idx, slot))
+                if idx == len(table) - 1:
+                    stage = tail.at[slot]
+                else:
+                    stage = (stage1, stage2)[which]
+                    staged = [pltpu.make_async_copy(landing(idx, slot, k), stage.at[k, pl.ds(0, rows)], stage_sem.at[which, k])
                               for k in range(len(targets))]
                     start_all(staged)
                     wait_all(staged)
-                    rows = stage.shape[1]
-                    base = lax.rem(idx, PARTS) * rows
-
-                    def some(i, inner):
-                        src = pl.ds(pl.multiple_of(i * 16, 16), 16)
-                        at = (layer, pl.ds(pl.multiple_of(base + i * 16, 16), 16))
-                        acc = p[at] + stage[0, src].astype(F32)
-                        acc = acc + stage[1, src].astype(F32)
-                        other = stage[2, src].astype(F32)
-                        acc = (acc + other) + other
-                        new = acc / 5.0 - total[at]
-                        p[at] = new
-                        pb[at] = new.astype(BF16)
-                        return inner
-                    lax.fori_loop(0, rows // 16, some, 0)
-
-                    @pl.when(window + 1 < windows)
-                    def _():
-                        start_all(sends(idx, 1 - slot, which))
-                return carry
-            lax.fori_loop(0, pieces, one, 0)
+
+                def some(i, carry):
+                    src = pl.ds(pl.multiple_of(i * 16, 16), 16)
+                    at = (layer, pl.ds(pl.multiple_of(start + i * 16, 16), 16))
+                    acc = p[at] + stage[0, src].astype(F32)
+                    acc = acc + stage[1, src].astype(F32)
+                    other = stage[2, src].astype(F32)
+                    acc = (acc + other) + other
+                    new = acc / 5.0 - total[at]
+                    p[at] = new
+                    pb[at] = new.astype(BF16)
+                    return carry
+                lax.fori_loop(0, rows // 16, some, 0)
+
+                @pl.when(window + 1 < windows)
+                def _():
+                    start_all(sends(idx, 1 - slot))
 
         def one_window(window, carry):
             local_step(2 * window, True, pb1, pb2)
@@ -223,7 +237,7 @@
     def device_program(w_in, w_out, inputs, targets):
         layers, dim, ff = w_in.shape[2:]
         steps, batch = inputs.shape[2:4]
-        pieces = layers * PARTS
+        pieces = len(exchange_table(layers, dim, ff))
         any_space = pl.BlockSpec(memory_space=pl.ANY)
         shape1, shape2 = (layers, dim, ff), (layers, ff, dim)
         sums = pl.pallas_call(
@@ -244,16 +258,36 @@
                 pltpu.VMEM((batch, dim), BF16),
                 pltpu.VMEM((batch, ff), BF16),
                 pltpu.VMEM((2, batch, dim), BF16), pltpu.VMEM((2, batch, dim), BF16),
-                pltpu.VMEM((3, dim // PARTS, ff), BF16), pltpu.VMEM((3, ff // PARTS, dim), BF16),
-                pltpu.SemaphoreType.DMA((pieces, 2)),
+                pltpu.VMEM((3, dim, ff), BF16), pltpu.VMEM((3, ff, dim), BF16),
+                pltpu.VMEM((2, 3, LAST_ROWS[-1], dim), BF16),
+                pltpu.SemaphoreType.DMA((pieces,)),
                 pltpu.SemaphoreType.DMA((2, 2)),
                 pltpu.SemaphoreType.DMA((2, 3)),
-                pltpu.SemaphoreType.DMA((pieces, 2, 3)),
-                pltpu.SemaphoreType.DMA((2, pieces, 2, 3)),
+                pltpu.SemaphoreType.DMA((pieces, 3)),
+                pltpu.SemaphoreType.DMA((2, pieces, 3)),
             ],
             compiler_params=pltpu.CompilerParams(collective_id=0, has_side_effects=True, vmem_limit_bytes=52_000_000),
         )(w_in[0, 0], w_out[0, 0], inputs[0, 0], targets[0, 0])
-        return sums[0][None, None], sums[1][None, None]
+
+        def store_kernel(p1, p2, out1, out2, sem):
+            copies = []
+            for idx in range(layers):
+                copies.append(pltpu.make_async_copy(p1.at[idx], out1.at[idx], sem.at[0, idx]))
+                copies.append(pltpu.make_async_copy(p2.at[idx], out2.at[idx], sem.at[1, idx]))
+            for copy in copies:
+                copy.start()
+            for copy in copies:
+                copy.wait()
+
+        new_in, new_out = pl.pallas_call(
+            store_kernel,
+            out_shape=[jax.ShapeDtypeStruct(shape1, F32), jax.ShapeDtypeStruct(shape2, F32)],
+            in_specs=[pl.BlockSpec(memory_space=pltpu.VMEM)] * 2,
+            out_specs=[any_space] * 2,
+            scratch_shapes=[pltpu.SemaphoreType.DMA((2, layers))],
+            compiler_params=pltpu.CompilerParams(vmem_limit_bytes=30_000_000),
+        )(sums[0], sums[1])
+        return new_in[None, None], new_out[None, None]
 
     block_spec = P("row", "col")
     return jax.shard_map(device_program, mesh=mesh,

time: 1100 us -> 1090 us (level)
  no operation moved by 1% of the time
where the time goes in v3:
time: 1090 us
  Pallas kernels  1090 us (100%)
    pallas_call x1, Pallas kernels, device_program(): pl.pallas_call(device_kernel, out_shape=[pltpu.VMEM(shape1, F32), pltpu.V...  1090 us

profile of v3, /device:TPU:0, one launch (start us, length us, event | category | flops | bytes accessed | tf_op | source)
XLA Modules:
  0.0 1090.8 jit_solution(14418452938360396800)
XLA Ops:
  0.6 1085.6 %shard_map.59 = (f32[3,512,1024]{2,1,0:T(8,128)S(1)}, f32[3,1024,512]{2,1,0:T(8,128)S(1)}, bf16[2,3,3,512,1024]{4,3,2,1,0:T(8,128)(2,1)}, bf16[2,3,3,1024,512]{4,3,2,1,0:T(8,128)(2,1)}) custom-call(f32[3,512,1024]{2,1,0:T(8,128)} %bitcast.8, f32[3,1024,512]{2,1,0:T(8,128)} %bitcast.9, bf16[16,512,512]{2,1,0:T(8,128)(2,1)} %bitcast.6, ...), custom_call_target="tpu_custom_call" | custom-call | tf_op jit(solution)/shard_map/pallas_call | solution.py:243
  1086.2 4.6 shard_map.60

commit v4 on v3

--- a/solution.py
+++ b/solution.py
@@ -15,8 +15,8 @@
 F32 = jnp.float32
 BF16 = jnp.bfloat16
 
-FIRST_ROWS = (64, 192)
-LAST_ROWS = (256, 128)
+FIRST_ROWS = (64,)
+LAST_ROWS = (256,)
 ROW_BLOCK = 256
 
 
@@ -38,9 +38,9 @@
 def solution(mesh):
     col_size = mesh.shape["col"]
 
-    def device_kernel(w1_hbm, w2_hbm, a_hbm, t_hbm, p1, p2, got1, got2,
+    def device_kernel(w1_hbm, w2_hbm, a_hbm, t_hbm, p1, p2, got1, got2, tail, tail_total,
                       sum1, sum2, pb1, pb2, qb1, qb2,
-                      hid, normed, slope, act, grad_h, grad_bf, d_pre, rows_buf, tgt_buf, stage1, stage2, tail,
+                      hid, normed, slope, act, grad_h, grad_bf, d_pre, rows_buf, tgt_buf, stage1, stage2,
                       load_sem, data_sem, stage_sem, send_sem, recv_sem):
         layers, dim, ff = p1.shape
         batch = rows_buf.shape[1]
@@ -200,6 +200,12 @@
 
             for idx, (which, layer, start, rows) in enumerate(table):
                 p, pb, total = params[which], bf_params[which], totals[which]
+                if idx == len(table) - 1:
+                    def keep(i, carry):
+                        at = pl.ds(pl.multiple_of(i * 32, 32), 32)
+                        tail_total[at] = total[layer, pl.ds(pl.multiple_of(start + i * 32, 32), 32)]
+                        return carry
+                    lax.fori_loop(0, rows // 32, keep, 0)
                 wait_all(sends(idx, slot))
                 if idx == len(table) - 1:
                     stage = tail.at[slot]
@@ -221,10 +227,13 @@
                     p[at] = new
                     pb[at] = new.astype(BF16)
                     return carry
-                lax.fori_loop(0, rows // 16, some, 0)
+                if idx < len(table) - 1:
+                    lax.fori_loop(0, rows // 16, some, 0)
 
                 @pl.when(window + 1 < windows)
                 def _():
+                    if idx == len(table) - 1:
+                        lax.fori_loop(0, rows // 16, some, 0)
                     start_all(sends(idx, 1 - slot))
 
         def one_window(window, carry):
@@ -243,9 +252,11 @@
         sums = pl.pallas_call(
             device_kernel,
             out_shape=[pltpu.VMEM(shape1, F32), pltpu.VMEM(shape2, F32),
-                       jax.ShapeDtypeStruct((2, 3) + shape1, BF16), jax.ShapeDtypeStruct((2, 3) + shape2, BF16)],
+                       jax.ShapeDtypeStruct((2, 3) + shape1, BF16), jax.ShapeDtypeStruct((2, 3) + shape2, BF16),
+                       pltpu.VMEM((2, 3, LAST_ROWS[-1], dim), BF16), pltpu.VMEM((LAST_ROWS[-1], dim), F32)],
             in_specs=[any_space] * 4,
-            out_specs=[pl.BlockSpec(memory_space=pltpu.VMEM)] * 2 + [any_space] * 2,
+            out_specs=([pl.BlockSpec(memory_space=pltpu.VMEM)] * 2 + [any_space] * 2
+                       + [pl.BlockSpec(memory_space=pltpu.VMEM)] * 2),
             scratch_shapes=[
                 pltpu.VMEM(shape1, F32), pltpu.VMEM(shape2, F32),
                 pltpu.VMEM(shape1, BF16), pltpu.VMEM(shape2, BF16),
@@ -259,7 +270,6 @@
                 pltpu.VMEM((batch, ff), BF16),
                 pltpu.VMEM((2, batch, dim), BF16), pltpu.VMEM((2, batch, dim), BF16),
                 pltpu.VMEM((3, dim, ff), BF16), pltpu.VMEM((3, ff, dim), BF16),
-                pltpu.VMEM((2, 3, LAST_ROWS[-1], dim), BF16),
                 pltpu.SemaphoreType.DMA((pieces,)),
                 pltpu.SemaphoreType.DMA((2, 2)),
                 pltpu.SemaphoreType.DMA((2, 3)),
@@ -269,24 +279,39 @@
             compiler_params=pltpu.CompilerParams(collective_id=0, has_side_effects=True, vmem_limit_bytes=52_000_000),
         )(w_in[0, 0], w_out[0, 0], inputs[0, 0], targets[0, 0])
 
-        def store_kernel(p1, p2, out1, out2, sem):
+        last_slot = (steps // 2 - 1) % 2
+
+        def store_kernel(p1, p2, tail, tail_total, out1, out2, last, sem):
+            rows = tail_total.shape[0]
             copies = []
             for idx in range(layers):
                 copies.append(pltpu.make_async_copy(p1.at[idx], out1.at[idx], sem.at[0, idx]))
-                copies.append(pltpu.make_async_copy(p2.at[idx], out2.at[idx], sem.at[1, idx]))
+                at = (idx, pl.ds(0, ff - rows if idx == layers - 1 else ff))
+                copies.append(pltpu.make_async_copy(p2.at[at], out2.at[at], sem.at[1, idx]))
             for copy in copies:
                 copy.start()
+
+            def some(i, carry):
+                src = pl.ds(pl.multiple_of(i * 16, 16), 16)
+                acc = p2[layers - 1, pl.ds(pl.multiple_of(ff - rows + i * 16, 16), 16)] + tail[last_slot, 0, src].astype(F32)
+                acc = acc + tail[last_slot, 1, src].astype(F32)
+                other = tail[last_slot, 2, src].astype(F32)
+                last[src] = ((acc + other) + other) / 5.0 - tail_total[src]
+                return carry
+            lax.fori_loop(0, rows // 16, some, 0)
+            copies.append(pltpu.make_async_copy(last, out2.at[layers - 1, pl.ds(ff - rows, rows)], sem.at[0, layers]))
+            copies[-1].start()
             for copy in copies:
                 copy.wait()
 
         new_in, new_out = pl.pallas_call(
             store_kernel,
             out_shape=[jax.ShapeDtypeStruct(shape1, F32), jax.ShapeDtypeStruct(shape2, F32)],
-            in_specs=[pl.BlockSpec(memory_space=pltpu.VMEM)] * 2,
+            in_specs=[pl.BlockSpec(memory_space=pltpu.VMEM)] * 4,
             out_specs=[any_space] * 2,
-            scratch_shapes=[pltpu.SemaphoreType.DMA((2, layers))],
+            scratch_shapes=[pltpu.VMEM((LAST_ROWS[-1], dim), F32), pltpu.SemaphoreType.DMA((2, layers + 1))],
             compiler_params=pltpu.CompilerParams(vmem_limit_bytes=30_000_000),
-        )(sums[0], sums[1])
+        )(sums[0], sums[1], sums[4], sums[5])
         return new_in[None, None], new_out[None, None]
 
     block_spec = P("row", "col")

time: 1090 us -> 1090 us (level)
  no operation moved by 1% of the time
where the time goes in v4:
time: 1090 us
  Pallas kernels  1090 us (100%)
    pallas_call x1, Pallas kernels, device_program(): pl.pallas_call(device_kernel, out_shape=[pltpu.VMEM(shape1, F32), pltpu.V...  1090 us

profile of v4, /device:TPU:0, one launch (start us, length us, event | category | flops | bytes accessed | tf_op | source)
XLA Modules:
  0.0 1090.5 jit_solution(2153658272258652973)
XLA Ops:
  0.6 1085.2 %shard_map.59 = (f32[3,512,1024]{2,1,0:T(8,128)S(1)}, f32[3,1024,512]{2,1,0:T(8,128)S(1)}, bf16[2,3,3,512,1024]{4,3,2,1,0:T(8,128)(2,1)}, bf16[2,3,3,1024,512]{4...) custom-call(f32[3,512,1024]{2,1,0:T(8,128)} %bitcast.8, f32[3,1024,512]{2,1,0:T(8,128)} %bitcast.9, ...), custom_call_target="tpu_custom_call" | custom-call | tf_op jit(solution)/shard_map/pallas_call | solution.py:252
  1085.9 4.6 shard_map.60

commit v5 on v4

--- a/solution.py
+++ b/solution.py
@@ -81,7 +81,7 @@
                     pltpu.make_async_copy(t_hbm.at[step], tgt_buf.at[slot], data_sem.at[slot, 1])]
 
         def start_all(copies):
-            for copy in copies:
+            for copy in reversed(copies):
                 copy.start()
 
         def wait_all(copies):

time: 1090 us -> 1090 us (level)
  no operation moved by 1% of the time
where the time goes in v5:
time: 1090 us
  Pallas kernels  1090 us (100%)
    pallas_call x1, Pallas kernels, device_program(): pl.pallas_call(device_kernel, out_shape=[pltpu.VMEM(shape1, F32), pltpu.V...  1090 us

profile of v5, /device:TPU:0, one launch (start us, length us, event | category | flops | bytes accessed | tf_op | source)
XLA Modules:
  0.0 1090.5 jit_solution(5156485187348797111)
XLA Ops:
  0.6 1085.2 %shard_map.59 = (f32[3,512,1024]{2,1,0:T(8,128)S(1)}, f32[3,1024,512]{2,1,0:T(8,128)S(1)}, bf16[2,3,3,512,1024]{4,3,2,1,0:T(8,128)(2,1)}, bf16[2,3,3,1024,512]{4...) custom-call(f32[3,512,1024]{2,1,0:T(8,128)} %bitcast.8, f32[3,1024,512]{2,1,0:T(8,128)} %bitcast.9, ...), custom_call_target="tpu_custom_call" | custom-call | tf_op jit(solution)/shard_map/pallas_call | solution.py:252
  1085.8 4.6 shard_map.60
